TPU v7x, 32 devices: a whole 2x2x4 slice. The times are simulated.
32 devices in a mesh: fsdp: 2 (over y), trow: 4 (over x, core), tcol: 4 (over z).
Axes of the slice: x: 2, y: 2, z: 4, core: 2. Of those that a mesh axis runs over, the one named last changes fastest.
Arguments:
- tokens: bfloat16 [512, 4096], P('fsdp', 'tcol'), may hold values from -100 to 100
- w_up: bfloat16 [4096, 16384], P('tcol', ('fsdp', 'trow')), may hold values from -0.1875 to 0.1875
- w_down: bfloat16 [16384, 4096], P(('fsdp', 'trow'), 'tcol'), may hold values from -0.046875 to 0.046875
- cotangent: bfloat16 [512, 4096], P('fsdp', 'tcol'), may hold values from -6 to 6
Outputs:
- mixed: bfloat16 [512, 4096], P('fsdp', 'tcol')
- input_gradient: bfloat16 [512, 4096], P('fsdp', 'tcol')
- grad_up: bfloat16 [4096, 16384], P('tcol', ('fsdp', 'trow'))
- grad_down: bfloat16 [16384, 4096], P(('fsdp', 'trow'), 'tcol')
All inputs are finite; a program needn't handle non-finite values.
Results may differ from a plain program's by a relative error of at most 0.02.
Values may be sent and summed in bfloat16 or wider, within the bound.
A program may use at most 128 MiB of HBM per device.

v0:
```python
import jax
import jax.numpy as jnp
from jax import lax
from jax.sharding import PartitionSpec as P


def gelu_value(pre):
    phi = 0.5 * (1.0 + jax.scipy.special.erf(pre * 0.7071067811865476))
    return pre * phi


def gelu_slope(pre):
    phi = 0.5 * (1.0 + jax.scipy.special.erf(pre * 0.7071067811865476))
    return phi + pre * jnp.exp(-0.5 * pre * pre) * 0.3989422804014327


def contract(left, right, left_dim, right_dim):
    return lax.dot_general(
        left, right, (((left_dim,), (right_dim,)), ((), ())), preferred_element_type=jnp.float32
    )


def local(tokens, w_up, w_down, cotangent):
    width = tokens.shape[1] * lax.axis_size("tcol")
    input_float = tokens.astype(jnp.float32)
    cot_all = lax.all_gather(cotangent, "fsdp", axis=0, tiled=True)
    sum_one, sum_two = lax.psum(
        (jnp.sum(input_float, axis=1), jnp.sum(input_float * input_float, axis=1)), "tcol"
    )
    token_mean = sum_one / width
    var = sum_two / width - token_mean * token_mean
    inverse_stddev = lax.rsqrt(var + 1e-05)
    centered_scaled = (input_float - token_mean[:, None]) * inverse_stddev[:, None]
    normalized_rows = centered_scaled.astype(jnp.bfloat16)
    normed_all = lax.all_gather(normalized_rows, "fsdp", axis=0, tiled=True)
    dhid_part = contract(cot_all, w_down, 1, 1).astype(jnp.bfloat16)
    dhid = lax.psum_scatter(dhid_part, "tcol", scatter_dimension=0, tiled=True).astype(jnp.float32)
    pre_part = contract(normed_all, w_up, 1, 0).astype(jnp.bfloat16)
    pre = lax.psum_scatter(pre_part, "tcol", scatter_dimension=0, tiled=True).astype(jnp.float32)
    hidden = lax.all_gather(gelu_value(pre).astype(jnp.bfloat16), "tcol", axis=0, tiled=True)
    dpre = lax.all_gather((dhid * gelu_slope(pre)).astype(jnp.bfloat16), "tcol", axis=0, tiled=True)
    branch_part = contract(hidden, w_down, 1, 0).astype(jnp.bfloat16)
    branch = lax.psum_scatter(branch_part, "fsdp", scatter_dimension=0, tiled=True)
    branch = lax.psum(branch, "trow").astype(jnp.float32)
    mixed = (input_float + branch).astype(jnp.bfloat16)
    grad_down = contract(hidden, cot_all, 0, 0).astype(jnp.bfloat16)
    dnorm_part = contract(dpre, w_up, 1, 1).astype(jnp.bfloat16)
    dnorm = lax.psum_scatter(dnorm_part, "fsdp", scatter_dimension=0, tiled=True)
    normed_gradient = lax.psum(dnorm, "trow").astype(jnp.float32)
    grad_up = contract(normed_all, dpre, 0, 0).astype(jnp.bfloat16)
    mean_first, mean_second = lax.psum(
        (jnp.sum(normed_gradient, axis=1), jnp.sum(normed_gradient * centered_scaled, axis=1)),
        "tcol",
    )
    first_moment = mean_first / width
    second_moment = mean_second / width
    input_gradient = cotangent.astype(jnp.float32) + inverse_stddev[:, None] * (
        normed_gradient - first_moment[:, None] - centered_scaled * second_moment[:, None]
    )
    return (mixed, input_gradient.astype(jnp.bfloat16), grad_up, grad_down)


def solution(mesh):
    return jax.shard_map(
        local,
        mesh=mesh,
        in_specs=(
            P("fsdp", "tcol"),
            P("tcol", ("fsdp", "trow")),
            P(("fsdp", "trow"), "tcol"),
            P("fsdp", "tcol"),
        ),
        out_specs=(
            P("fsdp", "tcol"),
            P("fsdp", "tcol"),
            P("tcol", ("fsdp", "trow")),
            P(("fsdp", "trow"), "tcol"),
        ),
        check_vma=False,
    )
```

profile of v0, /device:TPU:0, one launch (start us, length us, event | category | flops | bytes accessed | tf_op | source)
XLA Modules:
  0.0 359.4 jit_solution(15157938787356180238)
XLA Ops:
  7.2 1.3 convert_reduce_fusion
  8.5 13.5 %all-reduce.1 = (f32[256]{0:T(256)S(1)}, f32[256]{0:T(256)S(1)}) all-reduce(f32[256]{0:T(256)S(1)} %get-tuple-element.7, f32[256]{0:T(256)S(1)} %get-tuple-element.6), channel_id=1, replica_groups=mesh['fsdp'=2,'trow'=4,'tcol'=4] {'tcol'}, use_global_device_ids=true, to_apply=%region_3.0 | all-reduce | flops 512 | bytes 4096 | tf_op jit(solution)/shard_map/psum | solution.py:27
  22.0 2.1 fusion.7
  24.2 0.7 all-gather.9.cloned.1.call-update
  24.9 18.9 %all-gather.5.cloned.1.call-done = bf16[512,1024]{1,0:T(8,128)(2,1)} async-done(((bf16[256,1024]{1,0:T(8,128)(2,1)}), bf16[512,1024]{1,0:T(8,128)(2,1)}) %all-gather.5.cloned.1.call-update) | async-done | bytes 1048592 | tf_op jit(solution)/shard_map/all_gather | solution.py:35
  43.8 6.2 %convolution_convert_fusion.3 = bf16[512,2048]{1,0:T(8,128)(2,1)} fusion(bf16[512,1024]{1,0:T(8,128)(2,1)} %all-gather.5.cloned.1.call-done, bf16[1024,2048]{1,0:T(8,128)(2,1)} %param.5), kind=kOutput, calls=%fused_computation.3 | convolution fusion | flops 2148532224 | bytes 7340032 | tf_op jit(solution)/shard_map/dot_general | solution.py:18
  50.0 16.6 %all-gather.9.cloned.1.call-done = bf16[512,1024]{1,0:T(8,128)(2,1)} async-done(((bf16[256,1024]{1,0:T(8,128)(2,1)}), bf16[512,1024]{1,0:T(8,128)(2,1)}) %all-gather.9.cloned.1.call-update) | async-done | bytes 1048592 | tf_op jit(solution)/shard_map/all_gather | solution.py:26
  66.6 6.2 %convolution_convert_fusion.2 = bf16[512,2048]{1,0:T(8,128)(2,1)} fusion(bf16[512,1024]{1,0:T(8,128)(2,1)} %all-gather.9.cloned.1.call-done, bf16[2048,1024]{1,0:T(8,128)(2,1)} %param.6), kind=kOutput, calls=%fused_computation.2 | convolution fusion | flops 2148532224 | bytes 7340032 | tf_op jit(solution)/shard_map/dot_general | solution.py:18
  72.9 40.3 %reduce-scatter.5.cloned.1.call-done = bf16[128,2048]{1,0:T(8,128)(2,1)} async-done(((bf16[512,2048]{1,0:T(8,128)(2,1)}), bf16[128,2048]{1,0:T(8,128)(2,1)}) %reduce-scatter.5.cloned.1.call-update) | async-done | bytes 524304 | tf_op jit(solution)/shard_map/reduce_scatter | solution.py:39
  113.2 45.6 %reduce-scatter.9.cloned.1.call-done = bf16[128,2048]{1,0:T(8,128)(2,1)} async-done(((bf16[512,2048]{1,0:T(8,128)(2,1)}), bf16[128,2048]{1,0:T(8,128)(2,1)}) %reduce-scatter.9.cloned.1.call-update) | async-done | bytes 524304 | tf_op jit(solution)/shard_map/reduce_scatter | solution.py:37
  158.7 2.7 fusion.18
  161.5 0.5 all-gather.11.cloned.1.call-update
  162.1 44.4 %all-gather.7.cloned.1.call-done = bf16[512,2048]{1,0:T(8,128)(2,1)} async-done(((bf16[128,2048]{1,0:T(8,128)(2,1)}), bf16[512,2048]{1,0:T(8,128)(2,1)}) %all-gather.7.cloned.1.call-update) | async-done | bytes 2097168 | tf_op jit(solution)/shard_map/all_gather | solution.py:40
  206.5 6.1 %convolution_convert_fusion.5 = bf16[512,1024]{1,0:T(8,128)(2,1)} fusion(bf16[512,2048]{1,0:T(8,128)(2,1)} %all-gather.7.cloned.1.call-done, bf16[2048,1024]{1,0:T(8,128)(2,1)} %param.6), kind=kOutput, calls=%fused_computation.17 | convolution fusion | flops 2148007936 | bytes 7340032 | tf_op jit(solution)/shard_map/dot_general | solution.py:18
  212.7 40.3 %all-gather.11.cloned.1.call-done = bf16[512,2048]{1,0:T(8,128)(2,1)} async-done(((bf16[128,2048]{1,0:T(8,128)(2,1)}), bf16[512,2048]{1,0:T(8,128)(2,1)}) %all-gather.11.cloned.1.call-update) | async-done | bytes 2097168 | tf_op jit(solution)/shard_map/all_gather | solution.py:41
  253.0 6.2 %convolution_convert_fusion.4 = bf16[512,1024]{1,0:T(8,128)(2,1)} fusion(bf16[512,2048]{1,0:T(8,128)(2,1)} %all-gather.11.cloned.1.call-done, bf16[1024,2048]{1,0:T(8,128)(2,1)} %param.5), kind=kOutput, calls=%fused_computation.16 | convolution fusion | flops 2148007936 | bytes 7340032 | tf_op jit(solution)/shard_map/dot_general | solution.py:18
  259.4 15.6 %reduce-scatter.7.cloned.1.call-done = bf16[256,1024]{1,0:T(8,128)(2,1)} async-done(((bf16[512,1024]{1,0:T(8,128)(2,1)}), bf16[256,1024]{1,0:T(8,128)(2,1)}) %reduce-scatter.7.cloned.1.call-update) | async-done | bytes 524304 | tf_op jit(solution)/shard_map/reduce_scatter | solution.py:43
  275.0 23.2 %reduce-scatter.11.cloned.1.call-done = bf16[256,1024]{1,0:T(8,128)(2,1)} async-done(((bf16[512,1024]{1,0:T(8,128)(2,1)}), bf16[256,1024]{1,0:T(8,128)(2,1)}) %reduce-scatter.11.cloned.1.call-update) | async-done | bytes 524304 | tf_op jit(solution)/shard_map/reduce_scatter | solution.py:48
  298.3 4.4 %convolution_convert_fusion = bf16[2048,1024]{1,0:T(8,128)(2,1)} fusion(bf16[512,2048]{1,0:T(8,128)(2,1)S(1)} %copy-done.2, bf16[512,1024]{1,0:T(8,128)(2,1)S(1)} %copy-done.5), kind=kOutput, calls=%fused_computation | convolution fusion | flops 2149580800 | bytes 7340032 | tf_op jit(solution)/shard_map/dot_general | solution.py:18
  302.7 4.4 %convolution_convert_fusion.1 = bf16[1024,2048]{1,0:T(8,128)(2,1)} fusion(bf16[512,1024]{1,0:T(8,128)(2,1)S(1)} %copy-done.4, bf16[512,2048]{1,0:T(8,128)(2,1)S(1)} %copy-done.3), kind=kOutput, calls=%fused_computation.1 | convolution fusion | flops 2149580800 | bytes 7340032 | tf_op jit(solution)/shard_map/dot_general | solution.py:18
  307.2 29.9 %all-reduce.5.cloned.1.call-done = (bf16[256,1024]{1,0:T(8,128)(2,1)}, bf16[256,1024]{1,0:T(8,128)(2,1)}) async-done(((bf16[256,1024]{1,0:T(8,128)(2,1)}, bf16[256,1024]{1,0:T(8,128)(2,1)}), (bf16[256,1024]{1,0:T(8,128)(2,1)}, bf16[256,1024]{1,0:T(8,128)(2,1)})) %all-reduce.5.cloned.1.call-update) | async-done | bytes 1048592 | tf_op jit(solution)/shard_map/psum | solution.py:44
  337.1 1.5 convert_reduce_fusion.1
  338.5 11.7 %all-reduce = (f32[256]{0:T(256)S(1)}, f32[256]{0:T(256)S(1)}) all-reduce(f32[256]{0:T(256)S(1)} %get-tuple-element.5, f32[256]{0:T(256)S(1)} %get-tuple-element.4), channel_id=1, replica_groups=mesh['fsdp'=2,'trow'=4,'tcol'=4] {'tcol'}, use_global_device_ids=true, to_apply=%region_13.0 | all-reduce | flops 512 | bytes 4096 | tf_op jit(solution)/shard_map/psum | solution.py:51
  350.2 2.6 fusion.3
  (30 shorter events, 0.7 us)
Async XLA Ops:
  7.2 36.6 %all-gather.5.cloned.1.call-start = ((), (), s32[]{:S(2)}) async-start(), calls=%async_computation.4 | async-start | bytes 1572864 | tf_op jit(solution)/shard_map/all_gather | solution.py:35
  24.1 42.5 %all-gather.9.cloned.1.call-start = ((), (), s32[]{:S(2)}) async-start(), calls=%async_computation.8 | async-start | bytes 1572864 | tf_op jit(solution)/shard_map/all_gather | solution.py:26
  24.9 88.3 %reduce-scatter.5.cloned.1.call-start = ((), (), s32[]{:S(2)}) async-start(), calls=%async_computation.5 | async-start | bytes 2621440 | tf_op jit(solution)/shard_map/reduce_scatter | solution.py:39
  49.9 108.8 %reduce-scatter.9.cloned.1.call-start = ((), (), s32[]{:S(2)}) async-start(), calls=%async_computation.9 | async-start | bytes 2621440 | tf_op jit(solution)/shard_map/reduce_scatter | solution.py:37
  72.8 133.6 %all-gather.7.cloned.1.call-start = ((), (), s32[]{:S(2)}) async-start(), calls=%async_computation.6 | async-start | bytes 2621440 | tf_op jit(solution)/shard_map/all_gather | solution.py:40
  161.5 91.5 %all-gather.11.cloned.1.call-start = ((), (), s32[]{:S(2)}) async-start(), calls=%async_computation.10 | async-start | bytes 2621440 | tf_op jit(solution)/shard_map/all_gather | solution.py:41
  162.0 113.0 %reduce-scatter.7.cloned.1.call-start = ((), (), s32[]{:S(2)}) async-start(), calls=%async_computation.7 | async-start | bytes 1572864 | tf_op jit(solution)/shard_map/reduce_scatter | solution.py:43
  212.6 85.6 %copy-start.2 = (bf16[512,2048]{1,0:T(8,128)(2,1)S(1)}, bf16[512,2048]{1,0:T(8,128)(2,1)}, u32[]{:S(2)}) copy-start(bf16[512,2048]{1,0:T(8,128)(2,1)} %all-gather.7.cloned.1.call-done) | copy-start | bytes 6291460
  212.6 85.6 %copy-start.5 = (bf16[512,1024]{1,0:T(8,128)(2,1)S(1)}, bf16[512,1024]{1,0:T(8,128)(2,1)}, u32[]{:S(2)}) copy-start(bf16[512,1024]{1,0:T(8,128)(2,1)} %all-gather.9.cloned.1.call-done) | copy-start | bytes 3145732
  212.6 85.6 %reduce-scatter.11.cloned.1.call-start = ((), (), s32[]{:S(2)}) async-start(), calls=%async_computation.11 | async-start | bytes 1572864 | tf_op jit(solution)/shard_map/reduce_scatter | solution.py:48
  259.1 77.9 %all-reduce.5.cloned.1.call-start = ((), (), s32[]{:S(2)}) async-start(), calls=%async_computation.12 | async-start | bytes 2097152 | tf_op jit(solution)/shard_map/psum | solution.py:44
  298.3 4.4 %copy-start.3 = (bf16[512,2048]{1,0:T(8,128)(2,1)S(1)}, bf16[512,2048]{1,0:T(8,128)(2,1)}, u32[]{:S(2)}) copy-start(bf16[512,2048]{1,0:T(8,128)(2,1)} %all-gather.11.cloned.1.call-done) | copy-start | bytes 6291460
  298.3 4.4 %copy-start.4 = (bf16[512,1024]{1,0:T(8,128)(2,1)S(1)}, bf16[512,1024]{1,0:T(8,128)(2,1)}, u32[]{:S(2)}) copy-start(bf16[512,1024]{1,0:T(8,128)(2,1)} %all-gather.5.cloned.1.call-done) | copy-start | bytes 3145732
  302.7 34.3 %copy-start = (bf16[256,1024]{1,0:T(8,128)(2,1)S(1)}, bf16[256,1024]{1,0:T(8,128)(2,1)}, u32[]{:S(2)}) copy-start(bf16[256,1024]{1,0:T(8,128)(2,1)} %param.4) | copy-start | bytes 1572868
  302.7 47.5 %copy-start.1 = (bf16[256,1024]{1,0:T(8,128)(2,1)S(1)}, bf16[256,1024]{1,0:T(8,128)(2,1)}, u32[]{:S(2)}) copy-start(bf16[256,1024]{1,0:T(8,128)(2,1)} %param.7) | copy-start | bytes 1572868
Sparse Core Ops, SparseCore 0:
  24.2 19.4 all-gather.4
  45.3 21.2 all-gather.8
  69.5 43.6 reduce-scatter.4
  115.9 42.8 reduce-scatter.8
  161.6 44.8 all-gather.6
  208.5 44.4 all-gather.10
  255.8 19.1 reduce-scatter.6
  277.8 20.3 reduce-scatter.10
  300.7 36.3 all-reduce.4
where the time goes:
time: 360 us; the launch traced here: 359 us
  waiting for transfers between devices  276 us (77%)
  matrix products  33.5 us (9%)
  blocking collectives  25.2 us (7%)
  between operations  13.9 us (4%)
  other arithmetic  10.2 us (3%)
    reduce_scatter x1, waiting for transfers between devices, local(): lax.psum_scatter(dhid_part, 'tcol', scatter_dimension=0, tiled=True)  45.6 us
    all_gather x1, waiting for transfers between devices, local(): lax.all_gather(gelu_value(pre).astype(jnp.bfloat16), 'tcol', axis=0, tile...  44.4 us
    all_gather x1, waiting for transfers between devices, local(): lax.all_gather((dhid * gelu_slope(pre)).astype(jnp.bfloat16), 'tcol', axi...  40.3 us
    reduce_scatter x1, waiting for transfers between devices, local(): lax.psum_scatter(pre_part, 'tcol', scatter_dimension=0, tiled=True)  40.3 us
    dot_general x6, matrix products, contract(): lax.dot_general(left, right, (((left_dim,), (right_dim,)), ((), ())), pre...  33.5 us
    psum x1, waiting for transfers between devices, local(): branch = lax.psum(branch, 'trow').astype(jnp.float32)  29.9 us
    reduce_scatter x1, waiting for transfers between devices, local(): lax.psum_scatter(dnorm_part, 'fsdp', scatter_dimension=0, tiled=True)  23.2 us
    all_gather x1, waiting for transfers between devices, local(): normed_all = lax.all_gather(normalized_rows, 'fsdp', axis=0, tiled=True)  18.9 us
  transfers between devices with their start and end apart: 9, of which 9 were waited for; matrix products, arithmetic and copies ran while one was open for 9% of the time, Pallas kernels for 0%

commit v1 on v0

--- a/solution.py
+++ b/solution.py
@@ -2,6 +2,12 @@
 import jax.numpy as jnp
 from jax import lax
 from jax.sharding import PartitionSpec as P
+
+
+def laid_out(blocks, dim):
+    shape = list(blocks.shape[1:])
+    shape[dim] *= blocks.shape[0]
+    return jnp.moveaxis(blocks, 0, dim).reshape(shape)
 
 
 def gelu_value(pre):
@@ -38,7 +44,20 @@
     pre_part = contract(normed_all, w_up, 1, 0).astype(jnp.bfloat16)
     pre = lax.psum_scatter(pre_part, "tcol", scatter_dimension=0, tiled=True).astype(jnp.float32)
     hidden = lax.all_gather(gelu_value(pre).astype(jnp.bfloat16), "tcol", axis=0, tiled=True)
-    dpre = lax.all_gather((dhid * gelu_slope(pre)).astype(jnp.bfloat16), "tcol", axis=0, tiled=True)
+    array = (dhid * gelu_slope(pre)).astype(jnp.bfloat16)
+    length = lax.axis_size("tcol")
+    pairs = [(i, (i + 1) % length) for i in range(length)]
+    back = [(b, a) for a, b in pairs]
+    lower, upper = ([], [])
+    for lap in range(length - 1):
+        if lap % 2 == 0:
+            lower.append(lax.ppermute(lower[-1] if lower else array, "tcol", pairs))
+        else:
+            upper.append(lax.ppermute(upper[-1] if upper else array, "tcol", back))
+    parts = jnp.stack([*lower[::-1], array, *upper])
+    shift = lax.axis_index("tcol") - len(lower)
+    parts = parts[(jnp.arange(length) - shift) % length]
+    dpre = laid_out(parts, 0)
     branch_part = contract(hidden, w_down, 1, 0).astype(jnp.bfloat16)
     branch = lax.psum_scatter(branch_part, "fsdp", scatter_dimension=0, tiled=True)
     branch = lax.psum(branch, "trow").astype(jnp.float32)

time: 360 us -> 346 us (0.961)
  waiting for transfers between devices: 276 us -> 240 us
  starting transfers between devices: 0.54 us -> 18.4 us
    ppermute x0 -> x3, waiting for transfers between devices: none -> 47.2 us  [the longest x2 30.7 us: local(): lower.append(lax.ppermute(lower[-1] if lower else array, 'tcol', pairs))]
    all_gather x1, waiting for transfers between devices: 44.4 us -> 0.02 us  [local(): lax.all_gather(gelu_value(pre).astype(jnp.bfloat16), 'tcol', axis=0, tile...]
    all_gather x1 -> x0, waiting for transfers between devices: 40.3 us -> none  [local(): lax.all_gather((dhid * gelu_slope(pre)).astype(jnp.bfloat16), 'tcol', axi...]
    ppermute x0 -> x3, starting transfers between devices: none -> 17.9 us  [the longest x2 14.8 us: local(): lower.append(lax.ppermute(lower[-1] if lower else array, 'tcol', pairs))]
    reduce_scatter x1, waiting for transfers between devices: 15.6 us -> 23.2 us  [local(): lax.psum_scatter(branch_part, 'fsdp', scatter_dimension=0, tiled=True)]
    reduce_scatter x1, waiting for transfers between devices: 23.2 us -> 17.9 us  [local(): lax.psum_scatter(dnorm_part, 'fsdp', scatter_dimension=0, tiled=True)]
  transfers between devices with their start and end apart: 9 -> 11, of which waited for: 9 -> 10; matrix products, arithmetic and copies ran while one was open for 9% -> 11% of each run, Pallas kernels for 0% -> 0%
where the time goes in v1:
time: 346 us
  waiting for transfers between devices  240 us (69%)
  matrix products  33.5 us (10%)
  blocking collectives  25.2 us (7%)
  starting transfers between devices  18.4 us (5%)
  between operations  14.2 us (4%)
  other arithmetic  11.4 us (3%)
    reduce_scatter x1, waiting for transfers between devices, local(): lax.psum_scatter(dhid_part, 'tcol', scatter_dimension=0, tiled=True)  45.6 us
    reduce_scatter x1, waiting for transfers between devices, local(): lax.psum_scatter(pre_part, 'tcol', scatter_dimension=0, tiled=True)  40.3 us
    dot_general x6, matrix products, contract(): lax.dot_general(left, right, (((left_dim,), (right_dim,)), ((), ())), pre...  33.5 us
    ppermute x2, waiting for transfers between devices, local(): lower.append(lax.ppermute(lower[-1] if lower else array, 'tcol', pairs))  30.7 us
    psum x1, waiting for transfers between devices, local(): branch = lax.psum(branch, 'trow').astype(jnp.float32)  29.9 us
    reduce_scatter x1, waiting for transfers between devices, local(): lax.psum_scatter(branch_part, 'fsdp', scatter_dimension=0, tiled=True)  23.2 us
    all_gather x1, waiting for transfers between devices, local(): normed_all = lax.all_gather(normalized_rows, 'fsdp', axis=0, tiled=True)  18.9 us
    reduce_scatter x1, waiting for transfers between devices, local(): lax.psum_scatter(dnorm_part, 'fsdp', scatter_dimension=0, tiled=True)  17.9 us
  transfers between devices with their start and end apart: 11, of which 10 were waited for; matrix products, arithmetic and copies ran while one was open for 11% of the time, Pallas kernels for 0%

profile of v1, /device:TPU:0, one launch (start us, length us, event | category | flops | bytes accessed | tf_op | source)
XLA Modules:
  0.0 345.9 jit_solution(4506160823717079744)
XLA Ops:
  8.5 13.5 %all-reduce.1 = (f32[256]{0:T(256)S(1)}, f32[256]{0:T(256)S(1)}) all-reduce(f32[256]{0:T(256)S(1)} %get-tuple-element.7, f32[256]{0:T(256)S(1)} %get-tuple-element.6), channel_id=1, replica_groups=mesh['fsdp'=2,'trow'=4,'tcol'=4] {'tcol'}, use_global_device_ids=true, to_apply=%region_3.0 | all-reduce | flops 512 | bytes 4096 | tf_op jit(solution)/shard_map/psum | solution.py:33
  22.0 2.1 fusion.7
  24.9 18.9 %all-gather.4.cloned.1.call-done = bf16[512,1024]{1,0:T(8,128)(2,1)} async-done(((bf16[256,1024]{1,0:T(8,128)(2,1)}), bf16[512,1024]{1,0:T(8,128)(2,1)}) %all-gather.4.cloned.1.call-update) | async-done | bytes 1048592 | tf_op jit(solution)/shard_map/all_gather | solution.py:41
  43.8 6.2 %convolution_convert_fusion.3 = bf16[512,2048]{1,0:T(8,128)(2,1)} fusion(bf16[512,1024]{1,0:T(8,128)(2,1)} %all-gather.4.cloned.1.call-done, bf16[1024,2048]{1,0:T(8,128)(2,1)} %param.5), kind=kOutput, calls=%fused_computation.4 | convolution fusion | flops 2148532224 | bytes 7340032 | tf_op jit(solution)/shard_map/dot_general | solution.py:24
  50.0 16.6 %all-gather.8.cloned.1.call-done = bf16[512,1024]{1,0:T(8,128)(2,1)} async-done(((bf16[256,1024]{1,0:T(8,128)(2,1)}), bf16[512,1024]{1,0:T(8,128)(2,1)}) %all-gather.8.cloned.1.call-update) | async-done | bytes 1048592 | tf_op jit(solution)/shard_map/all_gather | solution.py:32
  66.6 6.2 %convolution_convert_fusion.2 = bf16[512,2048]{1,0:T(8,128)(2,1)} fusion(bf16[512,1024]{1,0:T(8,128)(2,1)} %all-gather.8.cloned.1.call-done, bf16[2048,1024]{1,0:T(8,128)(2,1)} %param.6), kind=kOutput, calls=%fused_computation.3 | convolution fusion | flops 2148532224 | bytes 7340032 | tf_op jit(solution)/shard_map/dot_general | solution.py:24
  72.9 40.3 %reduce-scatter.5.cloned.1.call-done = bf16[128,2048]{1,0:T(8,128)(2,1)} async-done(((bf16[512,2048]{1,0:T(8,128)(2,1)}), bf16[128,2048]{1,0:T(8,128)(2,1)}) %reduce-scatter.5.cloned.1.call-update) | async-done | bytes 524304 | tf_op jit(solution)/shard_map/reduce_scatter | solution.py:45
  113.2 45.6 %reduce-scatter.9.cloned.1.call-done = bf16[128,2048]{1,0:T(8,128)(2,1)} async-done(((bf16[512,2048]{1,0:T(8,128)(2,1)}), bf16[128,2048]{1,0:T(8,128)(2,1)}) %reduce-scatter.9.cloned.1.call-update) | async-done | bytes 524304 | tf_op jit(solution)/shard_map/reduce_scatter | solution.py:43
  158.7 2.5 fusion.18
  162.1 3.2 collective-permute-start.2
  165.2 17.8 %collective-permute-done = bf16[128,2048]{1,0:T(8,128)(2,1)S(1)} collective-permute-done((bf16[128,2048]{1,0:T(8,128)(2,1)S(1)}, bf16[128,2048]{1,0:T(8,128)(2,1)S(1)}, u32[]{:S(2)}, u32[]{:S(2)}) %collective-permute-start) | collective-permute-done | bytes 524320 | tf_op jit(solution)/shard_map/ppermute | solution.py:54
  183.0 14.1 %collective-permute-start.1 = (bf16[128,2048]{1,0:T(8,128)(2,1)S(1)}, bf16[128,2048]{1,0:T(8,128)(2,1)S(1)}, u32[]{:S(2)}, u32[]{:S(2)}) collective-permute-start(bf16[128,2048]{1,0:T(8,128)(2,1)S(1)} %collective-permute-done), channel_id=1, source_target_pairs={{0,1},{1,2},{2,3},{3,0},{4,5},{5,6},{6,7},{7,4},{8,9},{9,10},{10,1... | collective-permute-start | bytes 1572872 | tf_op jit(solution)/shard_map/ppermute | solution.py:54
  197.1 16.6 %collective-permute-done.2 = bf16[128,2048]{1,0:T(8,128)(2,1)S(1)} collective-permute-done((bf16[128,2048]{1,0:T(8,128)(2,1)S(1)}, bf16[128,2048]{1,0:T(8,128)(2,1)S(1)}, u32[]{:S(2)}, u32[]{:S(2)}) %collective-permute-start.2) | collective-permute-done | bytes 524320 | tf_op jit(solution)/shard_map/ppermute | solution.py:56
  213.7 12.8 %collective-permute-done.1 = bf16[128,2048]{1,0:T(8,128)(2,1)S(1)} collective-permute-done((bf16[128,2048]{1,0:T(8,128)(2,1)S(1)}, bf16[128,2048]{1,0:T(8,128)(2,1)S(1)}, u32[]{:S(2)}, u32[]{:S(2)}) %collective-permute-start.1) | collective-permute-done | bytes 524320 | tf_op jit(solution)/shard_map/ppermute | solution.py:54
  228.8 2.0 gather_fusion
  230.8 6.2 %convolution_convert_fusion.4 = bf16[512,1024]{1,0:T(8,128)(2,1)} fusion(bf16[512,2048]{1,0:T(8,128)(2,1)} %bitcast.19, bf16[1024,2048]{1,0:T(8,128)(2,1)} %param.5), kind=kOutput, calls=%fused_computation.18 | convolution fusion | flops 2148007936 | bytes 7340032 | tf_op jit(solution)/shard_map/dot_general | solution.py:24
  237.0 6.2 %convolution_convert_fusion.5 = bf16[512,1024]{1,0:T(8,128)(2,1)} fusion(bf16[512,2048]{1,0:T(8,128)(2,1)} %all-gather.6.cloned.1.call-done, bf16[2048,1024]{1,0:T(8,128)(2,1)} %param.6), kind=kOutput, calls=%fused_computation.19 | convolution fusion | flops 2148007936 | bytes 7340032 | tf_op jit(solution)/shard_map/dot_general | solution.py:24
  243.5 17.9 %reduce-scatter.11.cloned.1.call-done = bf16[256,1024]{1,0:T(8,128)(2,1)} async-done(((bf16[512,1024]{1,0:T(8,128)(2,1)}), bf16[256,1024]{1,0:T(8,128)(2,1)}) %reduce-scatter.11.cloned.1.call-update) | async-done | bytes 524304 | tf_op jit(solution)/shard_map/reduce_scatter | solution.py:67
  261.4 23.2 %reduce-scatter.7.cloned.1.call-done = bf16[256,1024]{1,0:T(8,128)(2,1)} async-done(((bf16[512,1024]{1,0:T(8,128)(2,1)}), bf16[256,1024]{1,0:T(8,128)(2,1)}) %reduce-scatter.7.cloned.1.call-update) | async-done | bytes 524304 | tf_op jit(solution)/shard_map/reduce_scatter | solution.py:62
  284.7 4.4 %convolution_convert_fusion.1 = bf16[1024,2048]{1,0:T(8,128)(2,1)} fusion(bf16[512,1024]{1,0:T(8,128)(2,1)S(1)} %copy-done.6, bf16[512,2048]{1,0:T(8,128)(2,1)S(1)} %bitcast.20), kind=kOutput, calls=%fused_computation.2 | convolution fusion | flops 2149580800 | bytes 7340032 | tf_op jit(solution)/shard_map/dot_general | solution.py:24
  289.1 4.4 %convolution_convert_fusion = bf16[2048,1024]{1,0:T(8,128)(2,1)} fusion(bf16[512,2048]{1,0:T(8,128)(2,1)S(1)} %copy-done.5, bf16[512,1024]{1,0:T(8,128)(2,1)S(1)} %copy-done.7), kind=kOutput, calls=%fused_computation.1 | convolution fusion | flops 2149580800 | bytes 7340032 | tf_op jit(solution)/shard_map/dot_general | solution.py:24
  293.5 29.9 %all-reduce.5.cloned.1.call-done = (bf16[256,1024]{1,0:T(8,128)(2,1)}, bf16[256,1024]{1,0:T(8,128)(2,1)}) async-done(((bf16[256,1024]{1,0:T(8,128)(2,1)}, bf16[256,1024]{1,0:T(8,128)(2,1)}), (bf16[256,1024]{1,0:T(8,128)(2,1)}, bf16[256,1024]{1,0:T(8,128)(2,1)})) %all-reduce.5.cloned.1.call-update) | async-done | bytes 1048592 | tf_op jit(solution)/shard_map/psum | solution.py:63
  324.8 11.7 %all-reduce = (f32[256]{0:T(256)S(1)}, f32[256]{0:T(256)S(1)}) all-reduce(f32[256]{0:T(256)S(1)} %get-tuple-element.5, f32[256]{0:T(256)S(1)} %get-tuple-element.4), channel_id=1, replica_groups=mesh['fsdp'=2,'trow'=4,'tcol'=4] {'tcol'}, use_global_device_ids=true, to_apply=%region_13.14 | all-reduce | flops 512 | bytes 4096 | tf_op jit(solution)/shard_map/psum | solution.py:70
  336.5 2.6 fusion.3
  (41 shorter events, 7.1 us)
Async XLA Ops:
  7.2 36.6 %all-gather.4.cloned.1.call-start = ((), (), s32[]{:S(2)}) async-start(), calls=%async_computation.4 | async-start | bytes 1572864 | tf_op jit(solution)/shard_map/all_gather | solution.py:41
  24.1 42.5 %all-gather.8.cloned.1.call-start = ((), (), s32[]{:S(2)}) async-start(), calls=%async_computation.8 | async-start | bytes 1572864 | tf_op jit(solution)/shard_map/all_gather | solution.py:32
  24.9 88.3 %reduce-scatter.5.cloned.1.call-start = ((), (), s32[]{:S(2)}) async-start(), calls=%async_computation.5 | async-start | bytes 2621440 | tf_op jit(solution)/shard_map/reduce_scatter | solution.py:45
  49.9 108.8 %reduce-scatter.9.cloned.1.call-start = ((), (), s32[]{:S(2)}) async-start(), calls=%async_computation.9 | async-start | bytes 2621440 | tf_op jit(solution)/shard_map/reduce_scatter | solution.py:43
  72.8 164.2 %all-gather.6.cloned.1.call-start = ((), (), s32[]{:S(2)}) async-start(), calls=%async_computation.6 | async-start | bytes 2621440 | tf_op jit(solution)/shard_map/all_gather | solution.py:46
  161.3 100.1 %reduce-scatter.11.cloned.1.call-start = ((), (), s32[]{:S(2)}) async-start(), calls=%async_computation.10 | async-start | bytes 1572864 | tf_op jit(solution)/shard_map/reduce_scatter | solution.py:67
  161.3 21.7 %collective-permute-start = (bf16[128,2048]{1,0:T(8,128)(2,1)S(1)}, bf16[128,2048]{1,0:T(8,128)(2,1)S(1)}, u32[]{:S(2)}, u32[]{:S(2)}) collective-permute-start(bf16[128,2048]{1,0:T(8,128)(2,1)S(1)} %get-tuple-element.16), channel_id=1, source_target_pairs={{0,1},{1,2},{2,3},{3,0},{4,5},{5,6},{6,7},{7,4},{8,9},{9,10},{10,1... | collective-permute-start | bytes 1572872 | tf_op jit(solution)/shard_map/ppermute | solution.py:54
  162.1 51.6 %collective-permute-start.2 = (bf16[128,2048]{1,0:T(8,128)(2,1)S(1)}, bf16[128,2048]{1,0:T(8,128)(2,1)S(1)}, u32[]{:S(2)}, u32[]{:S(2)}) collective-permute-start(bf16[128,2048]{1,0:T(8,128)(2,1)S(1)} %get-tuple-element.16), channel_id=1, source_target_pairs={{1,0},{2,1},{3,2},{0,3},{5,4},{6,5},{7,6},{4,7},{9,8},{10,9},{11,1... | collective-permute-start | bytes 1572872 | tf_op jit(solution)/shard_map/ppermute | solution.py:56
  183.0 43.5 %collective-permute-start.1 = (bf16[128,2048]{1,0:T(8,128)(2,1)S(1)}, bf16[128,2048]{1,0:T(8,128)(2,1)S(1)}, u32[]{:S(2)}, u32[]{:S(2)}) collective-permute-start(bf16[128,2048]{1,0:T(8,128)(2,1)S(1)} %collective-permute-done), channel_id=1, source_target_pairs={{0,1},{1,2},{2,3},{3,0},{4,5},{5,6},{6,7},{7,4},{8,9},{9,10},{10,1... | collective-permute-start | bytes 1572872 | tf_op jit(solution)/shard_map/ppermute | solution.py:54
  213.7 12.8 %copy-start.3 = (bf16[128,2048]{1,0:T(8,128)(2,1)}, bf16[128,2048]{1,0:T(8,128)(2,1)S(1)}, u32[]{:S(2)}) copy-start(bf16[128,2048]{1,0:T(8,128)(2,1)S(1)} %collective-permute-done.2) | copy-start | bytes 1572868
  226.5 0.8 copy-start.4
  236.9 47.7 %reduce-scatter.7.cloned.1.call-start = ((), (), s32[]{:S(2)}) async-start(), calls=%async_computation.7 | async-start | bytes 1572864 | tf_op jit(solution)/shard_map/reduce_scatter | solution.py:62
  237.0 47.6 %copy-start.6 = (bf16[512,1024]{1,0:T(8,128)(2,1)S(1)}, bf16[512,1024]{1,0:T(8,128)(2,1)}, u32[]{:S(2)}) copy-start(bf16[512,1024]{1,0:T(8,128)(2,1)} %all-gather.4.cloned.1.call-done) | copy-start | bytes 3145732
  243.2 41.4 %copy-start.1 = (bf16[4,128,2048]{2,1,0:T(8,128)(2,1)S(1)}, bf16[4,128,2048]{2,1,0:T(8,128)(2,1)}, u32[]{:S(2)}) copy-start(bf16[4,128,2048]{2,1,0:T(8,128)(2,1)} %gather_fusion) | copy-start | bytes 6291460
  243.3 80.1 %all-reduce.5.cloned.1.call-start = ((), (), s32[]{:S(2)}) async-start(), calls=%async_computation.11 | async-start | bytes 2097152 | tf_op jit(solution)/shard_map/psum | solution.py:63
  284.6 4.4 %copy-start.5 = (bf16[512,2048]{1,0:T(8,128)(2,1)S(1)}, bf16[512,2048]{1,0:T(8,128)(2,1)}, u32[]{:S(2)}) copy-start(bf16[512,2048]{1,0:T(8,128)(2,1)} %all-gather.6.cloned.1.call-done) | copy-start | bytes 6291460
  284.7 4.4 %copy-start.7 = (bf16[512,1024]{1,0:T(8,128)(2,1)S(1)}, bf16[512,1024]{1,0:T(8,128)(2,1)}, u32[]{:S(2)}) copy-start(bf16[512,1024]{1,0:T(8,128)(2,1)} %all-gather.8.cloned.1.call-done) | copy-start | bytes 3145732
  289.1 34.3 %copy-start = (bf16[256,1024]{1,0:T(8,128)(2,1)S(1)}, bf16[256,1024]{1,0:T(8,128)(2,1)}, u32[]{:S(2)}) copy-start(bf16[256,1024]{1,0:T(8,128)(2,1)} %param.4) | copy-start | bytes 1572868
  289.1 47.5 %copy-start.2 = (bf16[256,1024]{1,0:T(8,128)(2,1)S(1)}, bf16[256,1024]{1,0:T(8,128)(2,1)}, u32[]{:S(2)}) copy-start(bf16[256,1024]{1,0:T(8,128)(2,1)} %param.7) | copy-start | bytes 1572868
Sparse Core Ops, SparseCore 0:
  24.2 19.4 all-gather.3
  45.3 21.2 all-gather.7
  69.5 43.6 reduce-scatter.4
  115.9 42.8 reduce-scatter.8
  161.4 71.4 all-gather.5
  237.1 24.2 reduce-scatter.10
  264.2 20.3 reduce-scatter.6
  287.0 36.2 all-reduce.4
